TPU v7x, 32 devices: a whole 2x2x4 slice. The times are simulated.
32 devices in a mesh: dp: 2 (over core), row: 4 (over y, x), col: 4 (over z).
Axes of the slice: x: 2, y: 2, z: 4, core: 2. Of those that a mesh axis runs over, the one named last changes fastest.
Arguments:
- compressed: float32 [24576, 767], P(('dp', 'row', 'col')), may hold values from -6 to 6
- qkv_weight: bfloat16 [768, 3, 768], P('row', None, 'col'), may hold values from -0.21875 to 0.21875
- qkv_bias: bfloat16 [2, 768], P(None, 'col'), may hold values from -3 to 3
- proj_weight: bfloat16 [768, 768], P('row', 'col'), may hold values from -3 to 3
- proj_bias: bfloat16 [768], replicated, may hold values from -1.75 to 1.75
- attn_gain: bfloat16 [768], replicated, may hold values from 0.5 to 1.5
- mlp_gain: bfloat16 [768], replicated, may hold values from 0.5 to 1.5
- up_weight: bfloat16 [768, 3072], P('row', 'col'), may hold values from -0.21875 to 0.21875
- up_bias: bfloat16 [3072], P('col'), may hold values from -3 to 3
- down_weight: bfloat16 [768, 3072], P('row', 'col'), may hold values from -0.109375 to 0.109375
- down_bias: bfloat16 [768], replicated, may hold values from -1.75 to 1.75
- dealing: int32 [8, 3072], P(('dp', 'row')), may hold values from 0 to 3071, each once within a row
- seq_lengths: int32 [8, 3], P(('dp', 'row')), may hold values from 1 to 2048, 3072 in all within a row
- pad_offsets: int32 [8, 3], P(('dp', 'row')), may hold values from 0 to 255
- cotangent: float32 [24576, 767], P(('dp', 'row', 'col')), may hold values from -6 to 6
Outputs:
- layer_out: float32 [24576, 767], P(('dp', 'row', 'col'))
- input_grad: float32 [24576, 767], P(('dp', 'row', 'col'))
- qkv_weight_grad: float32 [768, 3, 768], P('row', None, 'col')
- qkv_bias_grad: float32 [2, 768], P(None, 'col')
- proj_weight_grad: float32 [768, 768], P('row', 'col')
- proj_bias_grad: float32 [768], replicated
- attn_gain_grad: float32 [768], replicated
- mlp_gain_grad: float32 [768], replicated
- up_weight_grad: float32 [768, 3072], P('row', 'col')
- up_bias_grad: float32 [3072], P('col')
- down_weight_grad: float32 [768, 3072], P('row', 'col')
- down_bias_grad: float32 [768], replicated
Inputs may be any that keep to these rules, and one draw needn't show every extreme that they name: `dealing`: each row is an ordering of 0 to 3071. `seq_lengths`: each row sums to 3072; the longest sequence of every bin has exactly 2048 tokens.
All inputs are finite; a program needn't handle non-finite values.
Results may differ from a plain program's by a relative error of at most 0.0072.
Values may be sent and summed in bfloat16 or wider, within the bound.
A program may use at most 192 MiB of HBM per device.

v0:
```python
from functools import partial

import jax
import jax.numpy as jnp
from jax import lax
from jax.sharding import PartitionSpec as P

HD = 64
QBLK = 512


EPS = 1e-05


def crms(values, gain_vec):
    return values * lax.rsqrt(jnp.mean(values * values, axis=-1, keepdims=True) + EPS) * gain_vec


def mask_parts(length_row, offset_row, bin_tokens):
    ends = jnp.cumsum(length_row)
    starts = ends - length_row
    position = jnp.arange(bin_tokens, dtype=jnp.int32)
    segment = jnp.sum((position[:, None] >= ends[None, :]).astype(jnp.int32), axis=1)
    picks = (segment[:, None] == jnp.arange(length_row.shape[0], dtype=jnp.int32)[None, :]).astype(
        jnp.int32
    )
    start_of = jnp.sum(picks * starts[None, :], axis=1)
    offset_of = jnp.sum(picks * offset_row[None, :], axis=1)
    return (position, segment, position - start_of >= offset_of)


def gather_norm(values):
    return lax.all_gather(values, "col", axis=0, tiled=True)


def gather_grads(values):
    return lax.all_gather(values, "col", axis=0, tiled=True)


def sum_branch(term_fn, share_rows):
    return lax.psum_scatter(
        term_fn(jnp.int32(0), share_rows * lax.axis_size("col")),
        "col",
        scatter_dimension=0,
        tiled=True,
    )


def sum_inputs(term_fn, share_rows):
    return lax.psum_scatter(
        term_fn(jnp.int32(0), share_rows * lax.axis_size("col")),
        "col",
        scatter_dimension=0,
        tiled=True,
    )


def centered(values):
    return values - jnp.mean(values, axis=1, keepdims=True)


def local(
    compressed,
    qkv_weight,
    qkv_bias,
    proj_weight,
    proj_bias,
    attn_gain,
    mlp_gain,
    up_weight,
    up_bias,
    down_weight,
    down_bias,
    dealing,
    seq_lengths,
    pad_offsets,
    cotangent,
):
    share_rows = compressed.shape[0]
    col_count = lax.axis_size("col")
    row_count = lax.axis_size("row")
    bin_tokens = share_rows * col_count
    heads_width = qkv_weight.shape[2]
    local_heads = heads_width // HD
    scale = HD ** (-0.5)
    blocks = bin_tokens // QBLK
    order_row = dealing[0]
    inverse_order = (
        jnp.zeros((bin_tokens,), jnp.int32)
        .at[order_row]
        .set(jnp.arange(bin_tokens, dtype=jnp.int32))
    )
    position, segment, valid = mask_parts(seq_lengths[0], pad_offsets[0], bin_tokens)
    qkv_local = qkv_weight.reshape(qkv_weight.shape[0], 3 * heads_width)
    qkv_rows, proj_rows, up_rows, down_rows = (
        lax.all_gather(qkv_local, "row", axis=0, tiled=True),
        lax.all_gather(proj_weight, "row", axis=0, tiled=True),
        lax.all_gather(up_weight, "row", axis=0, tiled=True),
        lax.all_gather(down_weight, "row", axis=0, tiled=True),
    )
    decompressed = jnp.concatenate(
        [compressed, -jnp.sum(compressed, axis=1, keepdims=True)], axis=1
    )
    normed_one_f, norm_one_back = jax.vjp(crms, decompressed, attn_gain.astype(jnp.float32))
    normed_one = normed_one_f.astype(jnp.bfloat16)
    normed_full = gather_norm(normed_one)
    projected = jnp.dot(normed_full, qkv_rows, preferred_element_type=jnp.float32).reshape(
        bin_tokens, 3, heads_width
    )
    bias_f = qkv_bias.astype(jnp.float32)
    query_heads = (
        (projected[:, 0] + bias_f[0])
        .astype(jnp.bfloat16)[order_row]
        .reshape(bin_tokens, local_heads, HD)
    )
    key_heads = projected[:, 1].astype(jnp.bfloat16)[order_row].reshape(bin_tokens, local_heads, HD)
    value_heads = (
        (projected[:, 2] + bias_f[1])
        .astype(jnp.bfloat16)[order_row]
        .reshape(bin_tokens, local_heads, HD)
    )

    def allowed_rows(first_row):
        row_pos = lax.dynamic_slice_in_dim(position, first_row, QBLK)
        row_seg = lax.dynamic_slice_in_dim(segment, first_row, QBLK)
        same_seq = row_seg[:, None] == segment[None, :]
        causal = position[None, :] <= row_pos[:, None]
        visible = valid[None, :] | (position[None, :] == row_pos[:, None])
        return (same_seq & causal & visible)[None]

    def forward_block(block_index):
        first_row = block_index * QBLK
        query_block = lax.dynamic_slice_in_dim(query_heads, first_row, QBLK)
        scores = (
            jnp.einsum("qhd,khd->hqk", query_block, key_heads, preferred_element_type=jnp.float32)
            * scale
        )
        scores = jnp.where(allowed_rows(first_row), scores, -jnp.inf)
        row_max = jnp.max(scores, axis=2, keepdims=True)
        weights_exp = jnp.exp(scores - row_max)
        row_total = jnp.sum(weights_exp, axis=2, keepdims=True)
        probs = (weights_exp / row_total).astype(jnp.bfloat16)
        mixed = jnp.einsum("hqk,khd->qhd", probs, value_heads, preferred_element_type=jnp.float32)
        return (mixed.astype(jnp.bfloat16), (row_max + jnp.log(row_total))[:, :, 0])

    attended, log_totals = lax.map(forward_block, jnp.arange(blocks, dtype=jnp.int32))
    attended_given = attended.reshape(bin_tokens, heads_width)[inverse_order]

    def attn_term(first_row, row_count_now):
        return jnp.einsum(
            "ti,oi->to", attended_given, proj_rows, preferred_element_type=jnp.float32
        )

    branch_one = sum_branch(attn_term, share_rows) + proj_bias.astype(jnp.float32)
    residual_two = decompressed + centered(branch_one)
    normed_two_f, norm_two_back = jax.vjp(crms, residual_two, mlp_gain.astype(jnp.float32))
    normed_two = normed_two_f.astype(jnp.bfloat16)
    gelu_fn = partial(jax.nn.gelu, approximate=True)
    normed_rows = gather_norm(normed_two)
    pre_act = jnp.dot(normed_rows, up_rows, preferred_element_type=jnp.float32) + up_bias.astype(
        jnp.float32
    )
    hidden_f, gelu_back = jax.vjp(gelu_fn, pre_act)
    hidden = hidden_f.astype(jnp.bfloat16)

    def hidden_term(first_row, row_count_now):
        picked = lax.dynamic_slice_in_dim(hidden, first_row, row_count_now)
        return jnp.einsum("tf,of->to", picked, down_rows, preferred_element_type=jnp.float32)

    branch_two = sum_branch(hidden_term, share_rows) + down_bias.astype(jnp.float32)
    residual_three = residual_two + centered(branch_two)
    layer_out = residual_three[:, :-1]
    grad_three = jnp.pad(cotangent, ((0, 0), (0, 1)))
    grad_two_out = centered(grad_three).astype(jnp.bfloat16)
    down_bias_grad = jnp.sum(grad_two_out.astype(jnp.float32), axis=0)
    grad_two_rows = gather_grads(grad_two_out)
    hidden_grad = jnp.dot(grad_two_rows, down_rows, preferred_element_type=jnp.float32)
    down_grad = jnp.einsum("to,tf->of", grad_two_rows, hidden, preferred_element_type=jnp.float32)
    pre_grad = gelu_back(hidden_grad)[0].astype(jnp.bfloat16)
    up_grad = jnp.einsum("td,tf->df", normed_rows, pre_grad, preferred_element_type=jnp.float32)
    up_bias_grad = jnp.sum(pre_grad.astype(jnp.float32), axis=0)

    def up_term(first_row, row_count_now):
        return jnp.einsum("tf,df->td", pre_grad, up_rows, preferred_element_type=jnp.float32)

    normed_two_grad = sum_inputs(up_term, share_rows)
    residual_norm_grad, mlp_gain_part = norm_two_back(normed_two_grad)
    residual_two_grad = grad_three + residual_norm_grad
    grad_one_out = centered(residual_two_grad).astype(jnp.bfloat16)
    proj_bias_grad = jnp.sum(grad_one_out.astype(jnp.float32), axis=0)
    grad_one_rows = gather_grads(grad_one_out)
    attended_grad = jnp.einsum(
        "to,oi->ti", grad_one_rows, proj_rows, preferred_element_type=jnp.float32
    ).astype(jnp.bfloat16)
    proj_grad = jnp.einsum(
        "to,ti->oi", grad_one_rows, attended_given, preferred_element_type=jnp.float32
    )
    attended_grad_heads = attended_grad[order_row].reshape(bin_tokens, local_heads, HD)

    def backward_block(carry, block_index):
        key_acc, value_acc = carry
        first_row = block_index * QBLK
        query_block = lax.dynamic_slice_in_dim(query_heads, first_row, QBLK)
        grad_block = lax.dynamic_slice_in_dim(attended_grad_heads, first_row, QBLK)
        log_block = log_totals[block_index]
        scores = (
            jnp.einsum("qhd,khd->hqk", query_block, key_heads, preferred_element_type=jnp.float32)
            * scale
        )
        probs_f = jnp.where(allowed_rows(first_row), jnp.exp(scores - log_block[:, :, None]), 0.0)
        probs_low = probs_f.astype(jnp.bfloat16)
        prob_grad = jnp.einsum(
            "qhd,khd->hqk", grad_block, value_heads, preferred_element_type=jnp.float32
        )
        row_dot = jnp.sum(probs_f * prob_grad, axis=2, keepdims=True)
        score_grad = (probs_f * (prob_grad - row_dot)).astype(jnp.bfloat16)
        query_grad = (
            jnp.einsum("hqk,khd->qhd", score_grad, key_heads, preferred_element_type=jnp.float32)
            * scale
        )
        key_acc = (
            key_acc
            + jnp.einsum(
                "hqk,qhd->khd", score_grad, query_block, preferred_element_type=jnp.float32
            )
            * scale
        )
        value_acc = value_acc + jnp.einsum(
            "hqk,qhd->khd", probs_low, grad_block, preferred_element_type=jnp.float32
        )
        return ((key_acc, value_acc), query_grad)

    zero_heads = jnp.zeros((bin_tokens, local_heads, HD), jnp.float32)
    (key_grad, value_grad), query_grads = lax.scan(
        backward_block, (zero_heads, zero_heads), jnp.arange(blocks, dtype=jnp.int32)
    )
    qkv_grad_proc = jnp.stack(
        [
            query_grads.reshape(bin_tokens, heads_width),
            key_grad.reshape(bin_tokens, heads_width),
            value_grad.reshape(bin_tokens, heads_width),
        ],
        axis=1,
    ).astype(jnp.bfloat16)
    qkv_grad_flat = qkv_grad_proc[inverse_order].reshape(bin_tokens, 3 * heads_width)
    qkv_grad_sum = jnp.sum(qkv_grad_flat.astype(jnp.float32), axis=0).reshape(3, heads_width)
    qkv_bias_part = jnp.concatenate([qkv_grad_sum[0], qkv_grad_sum[2]])
    qkv_rows_grad = jnp.einsum(
        "td,tk->dk", normed_full, qkv_grad_flat, preferred_element_type=jnp.float32
    )

    def qkv_term(first_row, row_count_now):
        return jnp.einsum("tk,dk->td", qkv_grad_flat, qkv_rows, preferred_element_type=jnp.float32)

    normed_one_grad = sum_inputs(qkv_term, share_rows)
    decompressed_norm_grad, attn_gain_part = norm_one_back(normed_one_grad)
    decompressed_grad = residual_two_grad + decompressed_norm_grad
    input_grad = decompressed_grad[:, :-1] - decompressed_grad[:, -1:]
    attn_gain_grad, mlp_gain_grad, proj_bias_total, down_bias_total = lax.psum(
        (attn_gain_part, mlp_gain_part, proj_bias_grad, down_bias_grad), ("dp", "row", "col")
    )
    qkv_bias_tile = jnp.broadcast_to(qkv_bias_part[None, :], (row_count, 2 * heads_width))
    up_bias_tile = jnp.broadcast_to(up_bias_grad[None, :], (row_count, up_bias_grad.shape[0]))
    row_sums = (
        lax.psum_scatter(qkv_rows_grad, "row", scatter_dimension=0, tiled=True),
        lax.psum_scatter(proj_grad, "row", scatter_dimension=0, tiled=True),
        lax.psum_scatter(up_grad, "row", scatter_dimension=0, tiled=True),
        lax.psum_scatter(down_grad, "row", scatter_dimension=0, tiled=True),
        lax.psum_scatter(qkv_bias_tile, "row", scatter_dimension=0, tiled=True),
        lax.psum_scatter(up_bias_tile, "row", scatter_dimension=0, tiled=True),
    )
    qkv_total, proj_total, up_total, down_total, qkv_bias_total, up_bias_total = lax.psum(
        (row_sums[0], row_sums[1], row_sums[2], row_sums[3], row_sums[4], row_sums[5]), "dp"
    )
    return (
        layer_out,
        input_grad,
        qkv_total.reshape(qkv_total.shape[0], 3, heads_width),
        qkv_bias_total.reshape(2, heads_width),
        proj_total,
        proj_bias_total,
        attn_gain_grad,
        mlp_gain_grad,
        up_total,
        up_bias_total.reshape(-1),
        down_total,
        down_bias_total,
    )


def solution(mesh):
    placed = (
        P(("dp", "row", "col"), None),
        P("row", None, "col"),
        P(None, "col"),
        P("row", "col"),
        P(),
        P(),
        P(),
        P("row", "col"),
        P("col"),
        P("row", "col"),
        P(),
        P(("dp", "row"), None),
        P(("dp", "row"), None),
        P(("dp", "row"), None),
        P(("dp", "row", "col"), None),
    )
    return jax.shard_map(
        local,
        mesh=mesh,
        in_specs=placed,
        out_specs=(
            P(("dp", "row", "col"), None),
            P(("dp", "row", "col"), None),
            P("row", None, "col"),
            P(None, "col"),
            P("row", "col"),
            P(),
            P(),
            P(),
            P("row", "col"),
            P("col"),
            P("row", "col"),
            P(),
        ),
        check_vma=False,
    )
```

profile of v0, /device:TPU:0, one launch (start us, length us, event | category | flops | bytes accessed | tf_op | source)
XLA Modules:
  0.0 2000.3 jit_solution(9084387599459261896)
XLA Ops:
  51.4 54.7 %all-gather.7.cloned.1.call-done = bf16[3072,768]{1,0:T(8,128)(2,1)} async-done(((bf16[768,768]{1,0:T(8,128)(2,1)}), bf16[3072,768]{1,0:T(8,128)(2,1)}) %all-gather.7.cloned.1.call-update) | async-done | bytes 4718608 | tf_op jit(solution)/shard_map/all_gather | solution.py:33
  155.9 135.0 %while.29 = (s32[]{:T(128)}, bf16[6,512,3,64]{1,3,2,0:T(8,128)(2,1)}, f32[6,3,512]{2,1,0:T(4,128)}, s32[6]{0:T(128)S(1)}, s32[3072]{0:T(1024)S(1)}, /*index=5*/s...) while((s32[]{:T(128)}, ...), condition=%wide.region_9.10_spmd.clone, body=%wide.region_6.0_spmd.clone.sunk | while | flops 1274116608 | bytes 65758424 | solution.py:146
  320.6 159.1 %reduce-scatter.9.cloned.1.call-done = f32[768,768]{1,0:T(8,128)} async-done(((f32[3072,768]{1,0:T(8,128)}), f32[768,768]{1,0:T(8,128)}) %reduce-scatter.9.cloned.1.call-update) | async-done | bytes 2359312 | tf_op jit(solution)/shard_map/reduce_scatter | solution.py:41
  489.8 87.3 %all-gather.9.cloned.1.call-done = bf16[3072,768]{1,0:T(8,128)(2,1)} async-done(((bf16[768,768]{1,0:T(8,128)(2,1)}), bf16[3072,768]{1,0:T(8,128)(2,1)}) %all-gather.9.cloned.1.call-update) | async-done | bytes 4718608 | tf_op jit(solution)/shard_map/all_gather | solution.py:33
  587.2 17.5 all-gather.13.cloned.1.call-done
  604.7 90.9 %all-gather.15.cloned.1.call-done = bf16[3072,768]{1,0:T(8,128)(2,1)} async-done(((bf16[768,768]{1,0:T(8,128)(2,1)}), bf16[3072,768]{1,0:T(8,128)(2,1)}) %all-gather.15.cloned.1.call-update) | async-done | bytes 4718608 | tf_op jit(solution)/shard_map/all_gather | solution.py:37
  695.5 15.4 convert_reduce_fusion.1
  730.0 149.1 %reduce-scatter.13.cloned.1.call-done = f32[768,768]{1,0:T(8,128)} async-done(((f32[3072,768]{1,0:T(8,128)}), f32[768,768]{1,0:T(8,128)}) %reduce-scatter.13.cloned.1.call-update) | async-done | bytes 2359312 | tf_op jit(solution)/shard_map/reduce_scatter | solution.py:50
  882.0 161.6 %reduce-scatter.11.cloned.1.call-done = f32[768,768]{1,0:T(8,128)} async-done(((f32[3072,768]{1,0:T(8,128)}), f32[768,768]{1,0:T(8,128)}) %reduce-scatter.11.cloned.1.call-update) | async-done | bytes 2359312 | tf_op jit(solution)/shard_map/reduce_scatter | solution.py:41
  1053.0 90.4 %all-gather.17.cloned.1.call-done = bf16[3072,768]{1,0:T(8,128)(2,1)} async-done(((bf16[768,768]{1,0:T(8,128)(2,1)}), bf16[3072,768]{1,0:T(8,128)(2,1)}) %all-gather.17.cloned.1.call-update) | async-done | bytes 4718608 | tf_op jit(solution)/shard_map/all_gather | solution.py:37
  1163.6 366.3 %while.30 = (s32[]{:T(128)}, f32[3072,3,64]{0,2,1:T(8,128)}, f32[3072,3,64]{0,2,1:T(8,128)}, bf16[6,512,3,64]{1,3,2,0:T(8,128)(2,1)}, s32[6]{0:T(128)S(1)}, /*in...) while((s32[]{:T(128)}, f32[3072,3,64]{0,2,1:T(8,128)}, ...), condition=%wide.region_22.23_spmd.clone.clone, body=%wide.region_20.22_spmd.clone.clone.sunk | while | flops 3103160832 | bytes 237585728 | solution.py:234
  1187.2 14.4 multiply_reduce_fusion.8
  1308.8 14.4 multiply_reduce_fusion.8
  1370.1 14.4 multiply_reduce_fusion.8
  1431.3 14.4 multiply_reduce_fusion.8
  1492.6 14.4 multiply_reduce_fusion.8
  1556.1 14.4 pad_maximum_fusion
  1570.4 27.3 %gather_fusion.5 = bf16[3072,3,192]{2,1,0:T(4,128)(2,1)} fusion(bf16[3072,3,192]{2,1,0:T(4,128)(2,1)} %pad_maximum_fusion, s32[3072]{0:T(1024)S(1)} %copy-done.28), kind=kCustom, calls=%fused_computation.5 | custom fusion | bytes 7090176 | tf_op jit(solution)/shard_map/gather | solution.py:245
  1649.4 38.7 %reduce-scatter.21.cloned.1.call-done = f32[192,768]{1,0:T(8,128)} async-done(((f32[768,768]{1,0:T(8,128)}), f32[192,768]{1,0:T(8,128)}) %reduce-scatter.21.cloned.1.call-update) | async-done | bytes 589840 | tf_op jit(solution)/shard_map/reduce_scatter | solution.py:267
  1688.1 40.2 %reduce-scatter.23.cloned.1.call-done = f32[192,768]{1,0:T(8,128)} async-done(((f32[768,768]{1,0:T(8,128)}), f32[192,768]{1,0:T(8,128)}) %reduce-scatter.23.cloned.1.call-update) | async-done | bytes 589840 | tf_op jit(solution)/shard_map/reduce_scatter | solution.py:268
  1728.3 29.0 %reduce-scatter.19.cloned.1.call-done = f32[192,192]{1,0:T(8,128)} async-done(((f32[768,192]{1,0:T(8,128)}), f32[192,192]{1,0:T(8,128)}) %reduce-scatter.19.cloned.1.call-update) | async-done | bytes 147472 | tf_op jit(solution)/shard_map/reduce_scatter | solution.py:266
  1778.8 15.2 all-reduce.4
  1800.7 142.8 %reduce-scatter.15.cloned.1.call-done = f32[768,768]{1,0:T(8,128)} async-done(((f32[3072,768]{1,0:T(8,128)}), f32[768,768]{1,0:T(8,128)}) %reduce-scatter.15.cloned.1.call-update) | async-done | bytes 2359312 | tf_op jit(solution)/shard_map/reduce_scatter | solution.py:50
  1949.3 41.4 %all-reduce.3 = (f32[768]{0:T(1024)}, f32[768]{0:T(1024)}, f32[768]{0:T(1024)}, f32[768]{0:T(1024)}) all-reduce(f32[768]{0:T(1024)S(1)} %copy-done.38, f32[768]{0:T(1024)S(1)} %get-tuple-element.332, f32[768]{0:T(1024)S(1)} %copy-done.37, f32[768]{0:T(1024)S(1)} %copy-done.36), channel_id=1, replica_groups=mesh['dp'=2,'row'=4,'col'=4] {'dp','row','col'}, use_global_device_ids=true, to_apply=%region_33.34 | all-reduce | flops 3072 | bytes 24576 | tf_op jit(solution)/shard_map/psum | solution.py:259
  (363 shorter events, 716.7 us)
Async XLA Ops:
  8.0 98.1 %all-gather.7.cloned.1.call-start = ((), (), s32[]{:S(2)}) async-start(), calls=%async_computation.8 | async-start | bytes 5898240 | tf_op jit(solution)/shard_map/all_gather | solution.py:33
  13.9 465.8 %reduce-scatter.9.cloned.1.call-start = ((), (), s32[]{:S(2)}) async-start(), calls=%async_computation.9 | async-start | bytes 11796480 | tf_op jit(solution)/shard_map/reduce_scatter | solution.py:41
  319.9 161.7 %copy-start.14 = (f32[768,1]{1,0:T(8,128)S(1)}, f32[768,1]{1,0:T(8,128)}, u32[]{:S(2)}) copy-start(f32[768,1]{1,0:T(8,128)} %copy-done.13) | copy-start | bytes 9220
  319.9 161.7 %copy-start.3 = (f32[768,767]{1,0:T(8,128)S(1)}, f32[768,767]{1,0:T(8,128)}, u32[]{:S(2)}) copy-start(f32[768,767]{1,0:T(8,128)} %param.19) | copy-start | bytes 7068676
  320.0 169.8 %all-gather.11.cloned.1.call-start = ((), (), s32[]{:S(2)}) async-start(), calls=%async_computation.11 | async-start | bytes 1474560 | tf_op jit(solution)/shard_map/all_gather | solution.py:98
  320.5 256.5 %all-gather.9.cloned.1.call-start = ((), (), s32[]{:S(2)}) async-start(), calls=%async_computation.10 | async-start | bytes 5898240 | tf_op jit(solution)/shard_map/all_gather | solution.py:33
  486.7 117.9 %all-gather.13.cloned.1.call-start = ((), (), s32[]{:S(2)}) async-start(), calls=%async_computation.12 | async-start | bytes 1474560 | tf_op jit(solution)/shard_map/all_gather | solution.py:99
  487.3 208.2 %all-gather.15.cloned.1.call-start = ((), (), s32[]{:S(2)}) async-start(), calls=%async_computation.14 | async-start | bytes 5898240 | tf_op jit(solution)/shard_map/all_gather | solution.py:37
  489.6 389.5 %reduce-scatter.13.cloned.1.call-start = ((), (), s32[]{:S(2)}) async-start(), calls=%async_computation.15 | async-start | bytes 11796480 | tf_op jit(solution)/shard_map/reduce_scatter | solution.py:50
  587.2 125.9 %copy-start.48 = (bf16[768,768]{1,0:T(8,128)(2,1)S(1)}, bf16[768,768]{1,0:T(8,128)(2,1)}, u32[]{:S(2)}) copy-start(bf16[768,768]{1,0:T(8,128)(2,1)} %all-gather.11.cloned.1.call-done) | copy-start | bytes 3538948
  719.4 324.2 %reduce-scatter.11.cloned.1.call-start = ((), (), s32[]{:S(2)}) async-start(), calls=%async_computation.13 | async-start | bytes 11796480 | tf_op jit(solution)/shard_map/reduce_scatter | solution.py:41
  729.3 149.8 %copy-start.6 = (f32[768,768]{1,0:T(8,128)S(1)}, f32[768,768]{1,0:T(8,128)}, u32[]{:S(2)}) copy-start(f32[768,768]{1,0:T(8,128)} %copy-done.5) | copy-start | bytes 7077892
  729.3 414.0 %all-gather.17.cloned.1.call-start = ((), (), s32[]{:S(2)}) async-start(), calls=%async_computation.16 | async-start | bytes 5898240 | tf_op jit(solution)/shard_map/all_gather | solution.py:37
  1052.9 594.4 %reduce-scatter.17.cloned.1.call-start = ((), (), s32[]{:S(2)}) async-start(), calls=%async_computation.18 | async-start | bytes 2457600 | tf_op jit(solution)/shard_map/reduce_scatter | solution.py:265
  1614.8 73.3 %reduce-scatter.21.cloned.1.call-start = ((), (), s32[]{:S(2)}) async-start(), calls=%async_computation.20 | async-start | bytes 2949120 | tf_op jit(solution)/shard_map/reduce_scatter | solution.py:267
  1623.9 104.4 %reduce-scatter.23.cloned.1.call-start = ((), (), s32[]{:S(2)}) async-start(), calls=%async_computation.21 | async-start | bytes 2949120 | tf_op jit(solution)/shard_map/reduce_scatter | solution.py:268
  1633.6 123.8 %reduce-scatter.19.cloned.1.call-start = ((), (), s32[]{:S(2)}) async-start(), calls=%async_computation.19 | async-start | bytes 983040 | tf_op jit(solution)/shard_map/reduce_scatter | solution.py:266
  1639.6 158.9 %all-reduce.9.cloned.1.call-start = ((), (), s32[]{:S(2)}) async-start(), calls=%async_computation.22 | async-start | bytes 3932160 | tf_op jit(solution)/shard_map/psum | solution.py:272
  1757.4 186.1 %reduce-scatter.15.cloned.1.call-start = ((), (), s32[]{:S(2)}) async-start(), calls=%async_computation.17 | async-start | bytes 11796480 | tf_op jit(solution)/shard_map/reduce_scatter | solution.py:50
  1770.2 173.3 %copy-start.4 = (f32[768,767]{1,0:T(8,128)S(1)}, f32[768,767]{1,0:T(8,128)}, u32[]{:S(2)}) copy-start(f32[768,767]{1,0:T(8,128)} %param.19) | copy-start | bytes 7068676
  1770.2 173.3 %copy-start.15 = (f32[768,1]{1,0:T(8,128)S(1)}, f32[768,1]{1,0:T(8,128)}, u32[]{:S(2)}) copy-start(f32[768,1]{1,0:T(8,128)} %copy-done.13) | copy-start | bytes 9220
  1770.2 173.3 %copy-start.31 = (f32[768]{0:T(1024)S(1)}, f32[768]{0:T(1024)}, u32[]{:S(2)}) copy-start(f32[768]{0:T(1024)} %copy-done.30) | copy-start | bytes 9220
  1770.2 173.3 %copy-start.33 = (f32[768]{0:T(1024)S(1)}, f32[768]{0:T(1024)}, u32[]{:S(2)}) copy-start(f32[768]{0:T(1024)} %copy-done.32) | copy-start | bytes 9220
  1800.7 145.4 %copy-start.35 = (f32[768]{0:T(1024)S(1)}, f32[768]{0:T(1024)}, u32[]{:S(2)}) copy-start(f32[768]{0:T(1024)} %copy-done.34) | copy-start | bytes 9220
  (49 other events, 612.8 us)
Sparse Core Ops, SparseCore 0:
  14.0 92.0 all-gather.6
  320.1 159.5 reduce-scatter.8
  1053.0 90.2 all-gather.16
  1757.5 21.2 all-reduce.8
  1781.0 162.4 reduce-scatter.14
Sparse Core Ops, SparseCore 1:
  322.3 25.8 all-gather.10
  486.8 90.2 all-gather.8
  578.8 25.8 all-gather.12
  606.3 89.2 all-gather.14
  719.5 159.6 reduce-scatter.12
  881.5 162.0 reduce-scatter.10
  1614.8 32.4 reduce-scatter.16
  1650.8 37.2 reduce-scatter.20
  1691.0 37.3 reduce-scatter.22
  1731.2 26.1 reduce-scatter.18
where the time goes:
time: 2010 us; the launch traced here: 2000 us
  waiting for transfers between devices  1070 us (53%)
  matrix products  376 us (19%)
  local copies, waits for them, and re-layouts  227 us (11%)
  other arithmetic  206 us (10%)
  blocking collectives  83.9 us (4%)
  loops' own time  20.4 us (1%)
    reduce_scatter x2, waiting for transfers between devices, sum_branch(): lax.psum_scatter(term_fn(jnp.int32(0), share_rows * lax.axis_size('col'))...  321 us
    reduce_scatter x2, waiting for transfers between devices, sum_inputs(): lax.psum_scatter(term_fn(jnp.int32(0), share_rows * lax.axis_size('col'))...  292 us
    all_gather x2, waiting for transfers between devices, gather_grads(): return lax.all_gather(values, 'col', axis=0, tiled=True)  181 us
    all_gather x2, waiting for transfers between devices, gather_norm(): return lax.all_gather(values, 'col', axis=0, tiled=True)  142 us
    dot_general x6, matrix products, backward_block(): jnp.einsum('qhd,khd->hqk', grad_block, value_heads, preferred_element_typ...  86.2 us
    convert_element_type x6, other arithmetic, backward_block(): score_grad = (probs_f * (prob_grad - row_dot)).astype(jnp.bfloat16)  83.7 us
    dot_general x6, matrix products, forward_block(): jnp.einsum('hqk,khd->qhd', probs, value_heads, preferred_element_type=jnp...  46.6 us
    dot_general x6, matrix products, backward_block(): jnp.einsum('hqk,qhd->khd', probs_low, grad_block, preferred_element_type=...  45.9 us
  transfers between devices with their start and end apart: 15, of which 13 were waited for; matrix products, arithmetic and copies ran while one was open for 5% of the time, Pallas kernels for 0%

commit v1 on v0

v1 whole, which is shorter than its diff:
```python
import functools

import jax
import jax.numpy as jnp
from jax import lax
from jax.experimental import pallas as pl
from jax.experimental.pallas import tpu as pltpu
from jax.sharding import PartitionSpec as P

HD = 64
EPS = 1e-05
NEG = -1e30
SCALE = HD ** (-0.5)
ALL = ("dp", "row", "col")
BF = jnp.bfloat16
F32 = jnp.float32
NN = (((1,), (0,)), ((), ()))
NT = (((1,), (1,)), ((), ()))


def mm(a, b, dims):
    return lax.dot_general(a, b, dims, preferred_element_type=F32)


def first_visible(length_row, offset_row, tokens):
    ends = jnp.cumsum(length_row)
    starts = ends - length_row
    position = jnp.arange(tokens, dtype=jnp.int32)
    segment = jnp.sum((position[:, None] >= ends[None, :]).astype(jnp.int32), axis=1)
    picks = (segment[:, None] == jnp.arange(length_row.shape[0], dtype=jnp.int32)[None, :]).astype(
        jnp.int32
    )
    first_real = jnp.sum(picks * (starts + offset_row)[None, :], axis=1)
    return jnp.where(position >= first_real, first_real, position)


def forward_kernel(heads, bk, first_ref, q_ref, k_ref, vt_ref, lo_ref, ot_ref, lse_ref):
    block = pl.program_id(0)
    bq = q_ref.shape[0]
    q0 = block * bq
    lo = lo_ref[...]
    queries = [q_ref[:, h * HD : (h + 1) * HD] for h in range(heads)]
    key_pos = lax.broadcasted_iota(jnp.int32, (bk, bq), 0)
    query_pos = q0 + lax.broadcasted_iota(jnp.int32, (bk, bq), 1)
    last = (q0 + bq - 1) // bk

    def step(i, carry):
        k0 = pl.multiple_of((last - i) * bk, bk)
        t = k0 + key_pos
        seen = (t >= lo) & (t <= query_pos)
        keys = k_ref[pl.ds(k0, bk), :]
        values = vt_ref[:, pl.ds(k0, bk)]
        out = []
        for h in range(heads):
            top, total, acc = carry[h]
            scores = mm(keys[:, h * HD : (h + 1) * HD], queries[h], NT)
            scores = jnp.where(seen, scores, NEG)
            top_new = jnp.maximum(top, jnp.max(scores, axis=0, keepdims=True))
            weights = jnp.exp(scores - top_new)
            fade = jnp.exp(top - top_new)
            total = total * fade + jnp.sum(weights, axis=0, keepdims=True)
            acc = acc * fade + mm(values[h * HD : (h + 1) * HD, :], weights.astype(BF), NN)
            out.append((top_new, total, acc))
        return tuple(out)

    start = tuple(
        (jnp.full((1, bq), NEG, F32), jnp.zeros((1, bq), F32), jnp.zeros((HD, bq), F32))
        for _ in range(heads)
    )
    result = lax.fori_loop(0, last - first_ref[block] + 1, step, start)
    for h in range(heads):
        top, total, acc = result[h]
        ot_ref[h * HD : (h + 1) * HD, :] = acc / total
        lse_ref[h : h + 1, :] = top + jnp.log(total)


def attend(q, k, vt, lo, bq=512, bk=512):
    n, w = q.shape
    heads = w // HD
    return pl.pallas_call(
        functools.partial(forward_kernel, heads, bk),
        out_shape=(jax.ShapeDtypeStruct((w, n), F32), jax.ShapeDtypeStruct((8, n), F32)),
        grid_spec=pltpu.PrefetchScalarGridSpec(
            num_scalar_prefetch=1,
            grid=(n // bq,),
            in_specs=[
                pl.BlockSpec((bq, w), lambda i, s: (i, 0)),
                pl.BlockSpec((n, w), lambda i, s: (0, 0)),
                pl.BlockSpec((w, n), lambda i, s: (0, 0)),
                pl.BlockSpec((1, bq), lambda i, s: (0, i)),
            ],
            out_specs=[
                pl.BlockSpec((w, bq), lambda i, s: (0, i)),
                pl.BlockSpec((8, bq), lambda i, s: (0, i)),
            ],
        ),
        cost_estimate=pl.CostEstimate(flops=10**10, bytes_accessed=10**7, transcendentals=10**7),
        name="attend",
    )(lo[::bq] // bk, q, k, vt, lo[None])


def backward_kernel(
    heads, bq, last_ref, k_ref, v_ref, kt_ref, q_ref, go_ref, lse_ref, dot_ref, lo_ref, out_ref, dq_ref
):
    block = pl.program_id(0)
    bk = k_ref.shape[0]
    w = heads * HD
    k0 = pl.multiple_of(block * bk, bk)

    @pl.when(block == 0)
    def _():
        dq_ref[...] = jnp.zeros_like(dq_ref)

    keys = [k_ref[:, h * HD : (h + 1) * HD] for h in range(heads)]
    values = [v_ref[:, h * HD : (h + 1) * HD] for h in range(heads)]
    keys_t = [kt_ref[h * HD : (h + 1) * HD, :] for h in range(heads)]
    t = k0 + lax.broadcasted_iota(jnp.int32, (bk, bq), 0)
    query_pos = lax.broadcasted_iota(jnp.int32, (bk, bq), 1)
    first = k0 // bq

    def step(i, carry):
        q0 = pl.multiple_of((first + i) * bq, bq)
        lo = lo_ref[:, pl.ds(q0, bq)]
        seen = (t >= lo) & (t <= query_pos + q0)
        q_block = q_ref[pl.ds(q0, bq), :]
        go_block = go_ref[pl.ds(q0, bq), :]
        lse = lse_ref[:, pl.ds(q0, bq)]
        dots = dot_ref[:, pl.ds(q0, bq)]
        out = []
        for h in range(heads):
            dk, dv = carry[h]
            q = q_block[:, h * HD : (h + 1) * HD]
            go = go_block[:, h * HD : (h + 1) * HD]
            scores = jnp.where(seen, mm(keys[h], q, NT) - lse[h : h + 1, :], NEG)
            probs = jnp.exp(scores)
            gp = mm(values[h], go, NT)
            gs = (probs * (gp - dots[h : h + 1, :])).astype(BF)
            dv = dv + mm(probs.astype(BF), go, NN)
            dk = dk + mm(gs, q, NN)
            dq_ref[h * HD : (h + 1) * HD, pl.ds(q0, bq)] += mm(keys_t[h], gs, NN)
            out.append((dk, dv))
        return tuple(out)

    zero = jnp.zeros((bk, HD), F32)
    result = lax.fori_loop(
        0, last_ref[block] - first + 1, step, tuple((zero, zero) for _ in range(heads))
    )
    for h in range(heads):
        out_ref[pl.ds(k0, bk), w + h * HD : w + (h + 1) * HD] = result[h][0].astype(BF)
        out_ref[pl.ds(k0, bk), 2 * w + h * HD : 2 * w + (h + 1) * HD] = result[h][1].astype(BF)

    @pl.when(block == pl.num_programs(0) - 1)
    def _():
        def turn(i, carry):
            at = pl.multiple_of(i * bq, bq)
            out_ref[pl.ds(at, bq), 0:w] = (dq_ref[:, pl.ds(at, bq)].T * SCALE).astype(BF)
            return carry

        lax.fori_loop(0, dq_ref.shape[1] // bq, turn, 0)


def attend_back(q, k, v, go, lse, dots, lo, bq=512, bk=256):
    n, w = q.shape
    heads = w // HD
    ends = (jnp.arange(n // bk, dtype=jnp.int32) + 1) * bk - 1
    last = (jnp.sum((lo[None, :] <= ends[:, None]).astype(jnp.int32), axis=1) - 1) // bq
    whole = lambda r, c: pl.BlockSpec((r, c), lambda i, s: (0, 0))
    return pl.pallas_call(
        functools.partial(backward_kernel, heads, bq),
        out_shape=jax.ShapeDtypeStruct((n, 3 * w), BF),
        grid_spec=pltpu.PrefetchScalarGridSpec(
            num_scalar_prefetch=1,
            grid=(n // bk,),
            in_specs=[
                pl.BlockSpec((bk, w), lambda i, s: (i, 0)),
                pl.BlockSpec((bk, w), lambda i, s: (i, 0)),
                pl.BlockSpec((w, bk), lambda i, s: (0, i)),
                whole(n, w),
                whole(n, w),
                whole(8, n),
                whole(8, n),
                whole(1, n),
            ],
            out_specs=whole(n, 3 * w),
            scratch_shapes=[pltpu.VMEM((w, n), F32)],
        ),
        cost_estimate=pl.CostEstimate(flops=2 * 10**10, bytes_accessed=10**7, transcendentals=10**7),
        name="attend_back",
    )(last, k, v, k.T, q, go, lse, dots, lo[None])


GELU_C = 0.7978845608028654
GELU_A = 0.044715


def middle_kernel(
    sizes,
    o_ref,
    proj_ref,
    x_ref,
    g3_ref,
    vec_ref,
    upb_ref,
    up_ref,
    down_ref,
    lay_ref,
    gx2_ref,
    go_ref,
    sums_ref,
    projg_ref,
    upbg_ref,
    grad_ref,
    x2_ref,
    n2_ref,
    n2t_ref,
    gy2_ref,
    gy2t_ref,
    y2_ref,
    gn2_ref,
    hid_ref,
    gu_ref,
    gy1_ref,
    gy1t_ref,
):
    groups, chunk = sizes
    step = pl.program_id(0)
    tokens, width = x_ref.shape
    gw = width // groups
    chunks = tokens // chunk
    proj_bias, gain, down_bias = vec_ref[0:1, :], vec_ref[1:2, :], vec_ref[2:3, :]

    @pl.when(step == 0)
    def _():
        def rows(i, carry):
            at = pl.ds(pl.multiple_of(i * chunk, chunk), chunk)
            y1 = mm(o_ref[0, at, :], proj_ref[:, 0:gw], NT)
            for g in range(1, groups):
                y1 += mm(o_ref[g, at, :], proj_ref[:, g * gw : (g + 1) * gw], NT)
            y1 += proj_bias
            x2 = x_ref[at, :] + (y1 - jnp.mean(y1, axis=1, keepdims=True))
            x2_ref[at, :] = x2
            r = lax.rsqrt(jnp.mean(x2 * x2, axis=1, keepdims=True) + EPS)
            n2_ref[at, :] = (x2 * r * gain).astype(BF)
            g3 = g3_ref[at, :]
            gy2 = (g3 - jnp.mean(g3, axis=1, keepdims=True)).astype(BF)
            gy2_ref[at, :] = gy2
            return carry + jnp.sum(gy2.astype(F32), axis=0, keepdims=True)

        sums_ref[...] = jnp.zeros_like(sums_ref)
        sums_ref[2:3, :] = lax.fori_loop(0, chunks, rows, jnp.zeros((1, width), F32))
        n2t_ref[...] = n2_ref[...].T
        gy2t_ref[...] = gy2_ref[...].T
        y2_ref[...] = jnp.zeros_like(y2_ref)
        gn2_ref[...] = jnp.zeros_like(gn2_ref)

    up = up_ref[...].reshape(width, up_ref.shape[-1])
    down = down_ref[...].reshape(width, down_ref.shape[-1])
    up_bias = upb_ref[0]

    def hidden(i, carry):
        at = pl.ds(pl.multiple_of(i * chunk, chunk), chunk)
        u = mm(n2_ref[at, :], up, NN) + up_bias
        square = u * u
        th = jnp.tanh(GELU_C * (u + GELU_A * (square * u)))
        hid = (0.5 * u * (1.0 + th)).astype(BF)
        hid_ref[at, :] = hid
        slope = 0.5 * (1.0 + th) + 0.5 * u * (1.0 - th * th) * (
            GELU_C * (1.0 + 3.0 * GELU_A * square)
        )
        gu = (mm(gy2_ref[at, :], down, NN) * slope).astype(BF)
        gu_ref[at, :] = gu
        y2_ref[at, :] += mm(hid, down, NT)
        gn2_ref[at, :] += mm(gu, up, NT)
        return carry + jnp.sum(gu.astype(F32), axis=0, keepdims=True)

    upbg_ref[0] = lax.fori_loop(0, chunks, hidden, jnp.zeros((1, up.shape[1]), F32))
    part = up_ref.shape[-2]
    blocks = width // part
    up_grad = mm(n2t_ref[...], gu_ref[...], NN).astype(BF)
    down_grad = mm(gy2t_ref[...], hid_ref[...], NN).astype(BF)
    grad_ref[0, :, 0, 0:part, :] = up_grad.reshape(blocks, part, up_grad.shape[1])
    grad_ref[0, :, 0, part : 2 * part, :] = down_grad.reshape(blocks, part, up_grad.shape[1])

    @pl.when(step == pl.num_programs(0) - 1)
    def _():
        def rows(i, carry):
            gain_sum, bias_sum = carry
            at = pl.ds(pl.multiple_of(i * chunk, chunk), chunk)
            x2 = x2_ref[at, :]
            y2 = y2_ref[at, :] + down_bias
            lay_ref[at, :] = (x2 + (y2 - jnp.mean(y2, axis=1, keepdims=True)))[:, 0 : width - 1]
            r = lax.rsqrt(jnp.mean(x2 * x2, axis=1, keepdims=True) + EPS)
            gn2 = gn2_ref[at, :]
            gain_sum = gain_sum + jnp.sum(gn2 * (x2 * r), axis=0, keepdims=True)
            gn2 = gn2 * gain
            gx2 = (
                g3_ref[at, :]
                + r * gn2
                - x2 * ((r * r * r) * jnp.mean(gn2 * x2, axis=1, keepdims=True))
            )
            gx2_ref[at, :] = gx2
            gy1 = (gx2 - jnp.mean(gx2, axis=1, keepdims=True)).astype(BF)
            gy1_ref[at, :] = gy1
            go = mm(gy1, proj_ref[...], NN).astype(BF)
            for g in range(groups):
                go_ref[g, at, :] = go[:, g * gw : (g + 1) * gw]
            return gain_sum, bias_sum + jnp.sum(gy1.astype(F32), axis=0, keepdims=True)

        zero = jnp.zeros((1, width), F32)
        gain_sum, bias_sum = lax.fori_loop(0, chunks, rows, (zero, zero))
        sums_ref[0:1, :] = gain_sum
        sums_ref[1:2, :] = bias_sum
        gy1t_ref[...] = gy1_ref[...].T
        for g in range(groups):
            projg_ref[:, g * gw : (g + 1) * gw] = mm(gy1t_ref[...], o_ref[g], NN).astype(BF)


def middle(o, proj, x, g3, vecs, up_bias, gathered, part):
    groups, tokens, gw = o.shape
    width = x.shape[1]
    halves, row_count, col_count, _, block = gathered.shape
    steps = halves * col_count
    chunk = 256
    once = pl.Buffered(buffer_count=1)
    whole = lambda *s: pl.BlockSpec(s, lambda i: (0,) * len(s), pipeline_mode=once)
    keep = lambda *s: pl.BlockSpec(s, lambda i: (0,) * len(s))
    wide = lambda which: pl.BlockSpec(
        (1, row_count, 1, part, block), lambda i: (i % halves, 0, i // halves, which, 0)
    )
    return pl.pallas_call(
        functools.partial(middle_kernel, (groups, chunk)),
        out_shape=(
            jax.ShapeDtypeStruct((tokens, width - 1), F32),
            jax.ShapeDtypeStruct((tokens, width), F32),
            jax.ShapeDtypeStruct((groups, tokens, gw), BF),
            jax.ShapeDtypeStruct((8, width), F32),
            jax.ShapeDtypeStruct((width, width), BF),
            jax.ShapeDtypeStruct((steps, 1, block), F32),
            jax.ShapeDtypeStruct((halves, row_count, col_count, 2 * part, block), BF),
        ),
        grid=(steps,),
        in_specs=[
            whole(groups, tokens, gw),
            whole(width, width),
            whole(tokens, width),
            whole(tokens, width),
            whole(8, width),
            pl.BlockSpec((1, 1, block), lambda i: (i, 0, 0)),
            wide(0),
            wide(1),
        ],
        out_specs=[
            keep(tokens, width - 1),
            keep(tokens, width),
            keep(groups, tokens, gw),
            keep(8, width),
            keep(width, width),
            pl.BlockSpec((1, 1, block), lambda i: (i, 0, 0)),
            pl.BlockSpec(
                (1, row_count, 1, 2 * part, block), lambda i: (i % halves, 0, i // halves, 0, 0)
            ),
        ],
        scratch_shapes=[
            pltpu.VMEM((tokens, width), F32),
            pltpu.VMEM((tokens, width), BF),
            pltpu.VMEM((width, tokens), BF),
            pltpu.VMEM((tokens, width), BF),
            pltpu.VMEM((width, tokens), BF),
            pltpu.VMEM((tokens, width), F32),
            pltpu.VMEM((tokens, width), F32),
            pltpu.VMEM((tokens, block), BF),
            pltpu.VMEM((tokens, block), BF),
            pltpu.VMEM((tokens, width), BF),
            pltpu.VMEM((width, tokens), BF),
        ],
        cost_estimate=pl.CostEstimate(flops=3 * 10**10, bytes_accessed=4 * 10**7, transcendentals=10**7),
        name="middle",
    )(o, proj, x, g3, vecs, up_bias, gathered, gathered)


def local(
    compressed,
    qkv_weight,
    qkv_bias,
    proj_weight,
    proj_bias,
    attn_gain,
    mlp_gain,
    up_weight,
    up_bias,
    down_weight,
    down_bias,
    dealing,
    seq_lengths,
    pad_offsets,
    cotangent,
):
    share = compressed.shape[0]
    dp_count, row_count, col_count = (lax.axis_size(a) for a in ALL)
    half = lax.axis_index("dp")
    tokens = share * col_count
    width = proj_weight.shape[0] * row_count
    part, hidden = up_weight.shape
    w = qkv_weight.shape[2]
    order = dealing[0]
    back = jnp.zeros((tokens,), jnp.int32).at[order].set(jnp.arange(tokens, dtype=jnp.int32))
    lo = first_visible(seq_lengths[0], pad_offsets[0], tokens)

    x = jnp.concatenate([compressed, -jnp.sum(compressed, axis=1, keepdims=True)], axis=1)
    gain1 = attn_gain.astype(F32)
    r1 = lax.rsqrt(jnp.mean(x * x, axis=-1, keepdims=True) + EPS)
    n1 = (x * r1 * gain1).astype(BF)
    g3 = jnp.pad(cotangent, ((0, 0), (0, 1)))

    qkv_rows = lax.all_gather(qkv_weight.reshape(part, 3 * w), "row", axis=0, tiled=True)
    n1_full = lax.all_gather(n1, "col", axis=0, tiled=True)

    block = hidden // dp_count
    cut = lambda a: lax.dynamic_slice_in_dim(a, half * block, block, 1)
    proj_half = lax.dynamic_slice_in_dim(proj_weight, half * (part // dp_count), part // dp_count, 0)
    mine = jnp.concatenate([cut(up_weight), cut(down_weight), proj_half.reshape(-1, block)], axis=0)
    mine, n1_full = lax.optimization_barrier((mine, n1_full))
    gathered = lax.all_gather(mine, ALL, axis=0, tiled=True).reshape(
        dp_count, row_count, col_count, mine.shape[0], block
    )
    proj = (
        gathered[:, :, :, 2 * part :, :]
        .reshape(dp_count, row_count, col_count, part // dp_count, w)
        .transpose(1, 0, 3, 2, 4)
        .reshape(width, width)
    )

    n1_proc = n1_full[order]
    bias = qkv_bias.astype(F32)
    q = (mm(n1_proc, qkv_rows[:, 0:w], NN) + bias[0]).astype(BF) * jnp.asarray(SCALE, BF)
    k = mm(n1_proc, qkv_rows[:, w : 2 * w], NN).astype(BF)
    v = (mm(n1_proc, qkv_rows[:, 2 * w :], NN) + bias[1]).astype(BF)
    ot, lse = attend(q, k, v.T, lo)
    o = ot.T
    o_given = o.astype(BF)[back].reshape(col_count, share, w)
    o_mine = lax.all_to_all(o_given, "col", 0, 0, tiled=True)

    vecs = jnp.pad(
        jnp.stack([proj_bias, mlp_gain, down_bias]).astype(F32), ((0, 5), (0, 0))
    )
    up_bias_all = lax.all_gather(up_bias, "col", axis=0, tiled=True).astype(F32)
    layer_out, gx2, go_mine, sums, proj_grad, up_bias_grad, wide_grad = middle(
        o_mine, proj, x, g3, vecs, up_bias_all.reshape(-1, 1, block), gathered, part
    )

    go_given = lax.all_to_all(go_mine, "col", 0, 0, tiled=True).reshape(tokens, w)
    proj_parts = (
        proj_grad.reshape(row_count, dp_count, part // dp_count, col_count, w)
        .transpose(1, 0, 3, 2, 4)
        .reshape(-1, w)
    )
    wide_sum = lax.psum_scatter(wide_grad.reshape(-1, block), ALL, scatter_dimension=0, tiled=True)
    proj_sum = lax.psum_scatter(proj_parts, ALL, scatter_dimension=0, tiled=True)
    wide_both = lax.all_gather(wide_sum, "dp", axis=0, tiled=False)
    up_total = jnp.concatenate([wide_both[i, 0:part] for i in range(dp_count)], axis=1).astype(F32)
    down_total = jnp.concatenate([wide_both[i, part:] for i in range(dp_count)], axis=1).astype(F32)
    proj_total = lax.all_gather(proj_sum, "dp", axis=0, tiled=True).astype(F32)
    small = jnp.concatenate([sums[0:3].reshape(1, -1), up_bias_grad.reshape(1, -1)], axis=1)
    small_total = jnp.sum(lax.all_gather(small, ALL, axis=0, tiled=True), axis=0)

    go = go_given[order]
    heads = w // HD
    dots = jnp.sum((go.astype(F32) * o).reshape(tokens, heads, HD), axis=2)
    dots = jnp.pad(dots.T, ((0, 8 - heads), (0, 0)))
    gqkv = attend_back(q, k, v, go, lse, dots, lo)

    qkv_grad = lax.dot_general(n1_proc, gqkv, (((0,), (0,)), ((), ())), preferred_element_type=F32)
    gain_part = jnp.sum(qkv_grad * qkv_rows.astype(F32), axis=1) / gain1
    bias_part = jnp.sum(gqkv.astype(F32), axis=0)
    tail = jnp.concatenate([gain_part, bias_part])[None]
    gn1_part = mm(gqkv[back], qkv_rows, NT).astype(BF)
    gn1 = lax.psum_scatter(gn1_part, "col", scatter_dimension=0, tiled=True).astype(F32)
    qkv_parts = (
        qkv_grad.astype(BF)
        .reshape(row_count, dp_count, part // dp_count, 3 * w)
        .transpose(1, 0, 2, 3)
        .reshape(width, 3 * w)
    )
    qkv_sum = lax.psum_scatter(qkv_parts, ("dp", "row"), scatter_dimension=0, tiled=True)
    qkv_total = lax.all_gather(qkv_sum, "dp", axis=0, tiled=True).astype(F32)
    tail_all = lax.all_gather(tail, ALL, axis=0, tiled=True)
    attn_gain_grad = jnp.sum(tail_all[:, 0:width], axis=0)
    col = lax.axis_index("col")
    bias_total = jnp.sum(
        lax.dynamic_index_in_dim(
            tail_all[:, width:].reshape(-1, col_count, 3 * w), col, 1, keepdims=False
        ),
        axis=0,
    )

    scaled = gn1 * gain1
    gx = gx2 + r1 * scaled - x * (r1**3 * jnp.mean(scaled * x, axis=1, keepdims=True))
    input_grad = gx[:, :-1] - gx[:, -1:]
    return (
        layer_out,
        input_grad,
        qkv_total.reshape(part, 3, w),
        jnp.stack([bias_total[0:w], bias_total[2 * w :]]),
        proj_total,
        small_total[width : 2 * width],
        attn_gain_grad,
        small_total[0:width],
        up_total,
        lax.dynamic_slice_in_dim(small_total, 3 * width + col * hidden, hidden, 0),
        down_total,
        small_total[2 * width : 3 * width],
    )


def solution(mesh):
    placed = (
        P(ALL, None),
        P("row", None, "col"),
        P(None, "col"),
        P("row", "col"),
        P(),
        P(),
        P(),
        P("row", "col"),
        P("col"),
        P("row", "col"),
        P(),
        P(("dp", "row"), None),
        P(("dp", "row"), None),
        P(("dp", "row"), None),
        P(ALL, None),
    )
    return jax.shard_map(
        local,
        mesh=mesh,
        in_specs=placed,
        out_specs=(
            P(ALL, None),
            P(ALL, None),
            P("row", None, "col"),
            P(None, "col"),
            P("row", "col"),
            P(),
            P(),
            P(),
            P("row", "col"),
            P("col"),
            P("row", "col"),
            P(),
        ),
        check_vma=False,
    )
```

time: 2010 us -> 849 us (0.42)
  waiting for transfers between devices: 1070 us -> 395 us
  matrix products: 376 us -> 28.4 us
  other arithmetic: 206 us -> 23.4 us
  Pallas kernels: 0 us -> 124 us
  local copies, waits for them, and re-layouts: 227 us -> 109 us
  blocking collectives: 83.9 us -> 122 us
  loops' own time: 20.4 us -> 0 us
    reduce_scatter x8 -> x4, waiting for transfers between devices: 728 us -> 261 us  [the longest x1 138 us: local(): lax.psum_scatter(wide_grad.reshape(-1, block), ALL, scatter_dimension=0,...]
    dot_general x54 -> x5, matrix products: 376 us -> 28.4 us  [the longest x4 21.7 us: mm(): return lax.dot_general(a, b, dims, preferred_element_type=F32)]
    all_gather x6 -> x2, waiting for transfers between devices: 341 us -> 91.2 us  [the longest x1 91.2 us: local(): n1_full = lax.all_gather(n1, 'col', axis=0, tiled=True)]
    pallas_call x0 -> x3, Pallas kernels: none -> 124 us  [the longest x1 54.2 us: middle(): pl.pallas_call(functools.partial(middle_kernel, (groups, chunk)), out_sha...]
    all_gather x2 -> x6, blocking collectives: 24.1 us -> 122 us  [the longest x1 70.3 us: local(): lax.all_gather(small, ALL, axis=0, tiled=True)]
    convert_element_type x14 -> x6, other arithmetic: 88.8 us -> 5.5 us  [the longest x1 1.82 us: local(): o_given = o.astype(BF)[back].reshape(col_count, share, w)]
    reduce_sum x18 -> x10, other arithmetic: 60 us -> 6.19 us  [the longest x1 1.85 us: local(): dots = jnp.sum((go.astype(F32) * o).reshape(tokens, heads, HD), axis=2)]
    psum x2 -> x0, blocking collectives: 44.5 us -> none  [the longest x1 41.4 us: local(): lax.psum((attn_gain_part, mlp_gain_part, proj_bias_grad, down_bias_grad),...]
  transfers between devices with their start and end apart: 15 -> 9, of which waited for: 13 -> 6; matrix products, arithmetic and copies ran while one was open for 5% -> 17% of each run, Pallas kernels for 0% -> 8%
where the time goes in v1:
time: 849 us; the launch traced here: 836 us
  waiting for transfers between devices  395 us (47%)
  Pallas kernels  124 us (15%)
  blocking collectives  122 us (14%)
  local copies, waits for them, and re-layouts  109 us (13%)
  matrix products  28.4 us (3%)
  other arithmetic  23.4 us (3%)
  starting transfers between devices  18.8 us (2%)
  between operations  14.9 us (2%)
    reduce_scatter x1, waiting for transfers between devices, local(): lax.psum_scatter(wide_grad.reshape(-1, block), ALL, scatter_dimension=0,...  138 us
    all_gather x1, waiting for transfers between devices, local(): n1_full = lax.all_gather(n1, 'col', axis=0, tiled=True)  91.2 us
    reduce_scatter x1, waiting for transfers between devices, local(): lax.psum_scatter(gn1_part, 'col', scatter_dimension=0, tiled=True)  84.1 us
    all_gather x1, blocking collectives, local(): lax.all_gather(small, ALL, axis=0, tiled=True)  70.3 us
    pallas_call x1, Pallas kernels, middle(): pl.pallas_call(functools.partial(middle_kernel, (groups, chunk)), out_sha...  54.2 us
    pallas_call x1, Pallas kernels, attend_back(): pl.pallas_call(functools.partial(backward_kernel, heads, bq), out_shape=j...  43.2 us
    reduce_scatter x1, waiting for transfers between devices, local(): lax.psum_scatter(qkv_parts, ('dp', 'row'), scatter_dimension=0, tiled=True)  39.1 us
    unnamed x8, waiting for transfers between devices  32.4 us
  transfers between devices with their start and end apart: 9, of which 6 were waited for; matrix products, arithmetic and copies ran while one was open for 17% of the time, Pallas kernels for 8%

profile of v1, /device:TPU:0, one launch (start us, length us, event | category | flops | bytes accessed | tf_op | source)
XLA Modules:
  0.0 835.7 jit_solution(17983878736647013513)
XLA Ops:
  13.8 91.2 %all-gather.7.cloned.1.call-done = bf16[3072,768]{1,0:T(8,128)(2,1)} async-done(((bf16[768,768]{1,0:T(8,128)(2,1)}), bf16[3072,768]{1,0:T(8,128)(2,1)}) %all-gather.7.cloned.1.call-update) | async-done | bytes 4718608 | tf_op jit(solution)/shard_map/all_gather | solution.py:416
  106.0 11.8 %scatter_custom_fusion = s32[3072]{0:T(1024)S(1)} fusion(s32[3072]{0:T(1024)S(1)} %bitcast.84, s32[3072]{0:T(1024)S(1)} %iota.30, s32[]{:T(128)} %constant.57.clone.1), kind=kCustom, calls=%fused_computation.58 | custom fusion | bytes 12292 | tf_op jit(solution)/shard_map/scatter | solution.py:406
  117.8 12.8 %all_gather.31 = bf16[768,576]{1,0:T(8,128)(2,1)S(1)} all-gather(bf16[192,576]{1,0:T(8,128)(2,1)S(1)} %copy.95), channel_id=1, replica_groups=mesh['dp'=2,'row'=4,'col'=4] {'row'}, dimensions={0}, use_global_device_ids=true | all-gather | bytes 1105920 | tf_op jit(solution)/shard_map/all_gather | solution.py:415
  131.8 17.5 %gather_fusion = bf16[3072,768]{1,0:T(8,128)(2,1)} fusion(bf16[3072,768]{1,0:T(8,128)(2,1)} %all-gather.7.cloned.1.call-done, s32[3072]{0:T(1024)S(1)} %broadcast_clamp_fusion), kind=kCustom, calls=%fused_computation | custom fusion | bytes 9449472 | tf_op jit(solution)/shard_map/gather | solution.py:433
  149.3 4.9 fusion.1.v_ref
  162.5 4.9 fusion.2.q_ref
  167.4 27.2 %attend.1 = (f32[192,3072]{1,0:T(8,128)}, f32[8,3072]{1,0:T(8,128)}) custom-call(s32[6]{0:T(128)} %and_select_fusion.1.first_ref, bf16[3072,192]{1,0:T(8,128)(2,1)} %fusion.2.q_ref, bf16[3072,192]{1,0:T(8,128)(2,1)} %copy.98.k_ref, bf16[192,3072]{1,0:T(8,128)(2,1)} %copy.99.vt_ref, s32[1,3072]{1,0:T(1,128)} %compare_select_fusion.lo_ref), custom_call_target="tpu_custom_call" | custom-call | flops 10000000000 | bytes 10000000 | tf_op jit(solution)/shard_map/attend/pallas_call | solution.py:80
  197.0 11.1 %gather_fusion.1 = bf16[3072,192]{1,0:T(8,128)(2,1)S(1)} fusion(bf16[3072,192]{1,0:T(8,128)(2,1)S(1)} %copy.100, s32[3072]{0:T(1024)S(1)} %fusion.12), kind=kCustom, calls=%fused_computation.1 | custom fusion | bytes 2371584 | tf_op jit(solution)/shard_map/gather | solution.py:440
  209.6 4.8 all-to-all-start
  217.8 31.9 %all-gather.2 = bf16[4,1,768]{2,1,0:T(2,128)(2,1)S(1)} all-gather(bf16[1,1,768]{2,1,0:T(2,128)(2,1)S(1)} %reshape.248), channel_id=1, replica_groups=mesh['dp'=2,'row'=4,'col'=4] {'col'}, dimensions={0}, use_global_device_ids=true | all-gather | bytes 7680 | tf_op jit(solution)/shard_map/all_gather | solution.py:446
  258.3 54.2 %middle.1 = (f32[768,767]{1,0:T(8,128)}, f32[768,768]{1,0:T(8,128)}, bf16[4,768,192]{2,1,0:T(8,128)(2,1)}, f32[8,768]{1,0:T(8,128)}, bf16[768,768]{1,0:T(8,128)(...) custom-call(bf16[4,768,192]{2,1,0:T(8,128)(2,1)} %copy.103.o_ref, bf16[768,768]{1,0:T(8,128)(2,1)} %reshape.183.proj_ref, ...), custom_call_target="tpu_custom_call" | custom-call | flops 30000001024 | bytes 40000000 | tf_op jit(solution)/shard_map/middle/pallas_call | solution.py:330
  315.0 4.3 all-to-all-start.1
  326.4 9.5 %all-reduce.6.cloned.1.call-start = ((), (), s32[]{:S(2)}) async-start(), calls=%async_computation.12 | async-start | bytes 344064
  335.9 10.4 %all-to-all-done.1 = bf16[4,768,192]{1,2,0:T(8,128)(2,1)} async-done(((bf16[4,768,192]{1,2,0:T(8,128)(2,1)}), bf16[4,768,192]{1,2,0:T(8,128)(2,1)}, u32[]{:S(2)}, u32[]{:S(2)}) %all-to-all-start.1) | async-done | bytes 1179680 | tf_op jit(solution)/shard_map/all_to_all | solution.py:451
  347.9 12.9 %gather_fusion.2 = bf16[3072,192]{1,0:T(8,128)(2,1)} fusion(bf16[3072,192]{1,0:T(8,128)(2,1)S(1)} %bitcast.65, s32[3072]{0:T(1024)S(1)} %broadcast_clamp_fusion), kind=kCustom, calls=%fused_computation.2 | custom fusion | bytes 2371584 | tf_op jit(solution)/shard_map/gather | solution.py:466
  368.9 43.2 %attend_back.1 = bf16[3072,576]{1,0:T(8,128)(2,1)} custom-call(s32[12]{0:T(128)} %and_select_fusion.last_ref, bf16[3072,192]{1,0:T(8,128)(2,1)} %copy.98.k_ref, bf16[3072,192]{1,0:T(8,128)(2,1)} %fusion.1.v_ref, bf16[192,3072]{1,0:T(8,128)(2,1)} %bitcast.66, bf16[3072,192]{1,0:T(8,128)(2,1)} %fusion.2.q_ref, bf16[3072,192]{1,0:T(8,128)(2,1)} %gather_fusion.2, ...), custom_call_target="tpu_custom_call" | custom-call | flops 20000000000 | bytes 10000000 | tf_op jit(solution)/shard_map/attend_back/pallas_call | solution.py:168
  412.1 6.7 multiply_reduce_fusion.2
  422.2 16.4 %gather_fusion.3 = bf16[3072,576]{1,0:T(8,128)(2,1)} fusion(bf16[3072,576]{1,0:T(8,128)(2,1)} %attend_back.1, s32[3072]{0:T(1024)S(1)} %fusion.12), kind=kCustom, calls=%fused_computation.3 | custom fusion | bytes 7090176 | tf_op jit(solution)/shard_map/gather | solution.py:476
  438.6 7.7 convolution_convert_fusion
  447.2 70.3 %all-gather.3 = f32[32,1,5376]{2,1,0:T(1,128)S(1)} all-gather(f32[1,1,5376]{2,1,0:T(1,128)S(1)} %maximum_bitcast_fusion), channel_id=1, replica_groups=mesh['dp'=2,'row'=4,'col'=4] {'dp','row','col'}, dimensions={0}, use_global_device_ids=true | all-gather | bytes 709632 | tf_op jit(solution)/shard_map/all_gather | solution.py:464
  521.3 31.6 %all-reduce.6.cloned.1.call-done = f32[43008]{0:T(1024)} async-done(((f32[43008]{0:T(1024)}), f32[43008]{0:T(1024)}) %all-reduce.6.cloned.1.call-update) | async-done | bytes 172048
  555.2 39.1 %reduce-scatter.7.cloned.1.call-done = bf16[96,576]{1,0:T(8,128)(2,1)} async-done(((bf16[768,576]{1,0:T(8,128)(2,1)}), bf16[96,576]{1,0:T(8,128)(2,1)}) %reduce-scatter.7.cloned.1.call-update) | async-done | bytes 110608 | tf_op jit(solution)/shard_map/reduce_scatter | solution.py:484
  597.8 84.1 %reduce-scatter.5.cloned.1.call-done = bf16[768,768]{1,0:T(8,128)(2,1)} async-done(((bf16[3072,768]{1,0:T(8,128)(2,1)}), bf16[768,768]{1,0:T(8,128)(2,1)}) %reduce-scatter.5.cloned.1.call-update) | async-done | bytes 1179664 | tf_op jit(solution)/shard_map/reduce_scatter | solution.py:477
  686.7 137.8 %reduce-scatter.11.cloned.1.call-done = bf16[384,384]{1,0:T(8,128)(2,1)} async-done(((bf16[12288,384]{1,0:T(8,128)(2,1)}), bf16[384,384]{1,0:T(8,128)(2,1)}) %reduce-scatter.11.cloned.1.call-update) | async-done | bytes 294928 | tf_op jit(solution)/shard_map/reduce_scatter | solution.py:457
  (160 shorter events, 74.7 us)
Async XLA Ops:
  7.2 5.7 copy-start
  7.2 97.8 %all-gather.7.cloned.1.call-start = ((), (), s32[]{:S(2)}) async-start(), calls=%async_computation.6 | async-start | bytes 5898240 | tf_op jit(solution)/shard_map/all_gather | solution.py:416
  12.7 92.3 %copy-start.14 = (bf16[192,3,192]{2,0,1:T(8,128)(2,1)S(1)}, bf16[192,3,192]{2,0,1:T(8,128)(2,1)}, u32[]{:S(2)}) copy-start(bf16[192,3,192]{2,0,1:T(8,128)(2,1)} %param.16) | copy-start | bytes 663556
  12.7 92.7 %copy-start.27 = (s32[1,3]{1,0:T(1,128)S(1)}, s32[1,3]{1,0:T(1,128)}, u32[]{:S(2)}) copy-start(s32[1,3]{1,0:T(1,128)} %param.27) | copy-start | bytes 40
  12.7 93.0 %copy-start.26 = (s32[1,3]{1,0:T(1,128)S(1)}, s32[1,3]{1,0:T(1,128)}, u32[]{:S(2)}) copy-start(s32[1,3]{1,0:T(1,128)} %param.28) | copy-start | bytes 40
  12.7 93.2 %copy-start.17 = (s32[1,3072]{1,0:T(1,128)S(1)}, s32[1,3072]{1,0:T(1,128)}, u32[]{:S(2)}) copy-start(s32[1,3072]{1,0:T(1,128)} %param.26) | copy-start | bytes 36868
  12.8 118.4 %copy-start.21 = (bf16[2,192]{1,0:T(2,128)(2,1)S(1)}, bf16[2,192]{1,0:T(2,128)(2,1)}, u32[]{:S(2)}) copy-start(bf16[2,192]{1,0:T(2,128)(2,1)} %param.17) | copy-start | bytes 2308
  12.8 239.7 %all-gather.9.cloned.1.call-start = ((), (), s32[]{:S(2)}) async-start(), calls=%async_computation.7 | async-start | bytes 10948608 | tf_op jit(solution)/shard_map/all_gather | solution.py:423
  130.6 31.8 %copy-start.8 = (bf16[768,576]{1,0:T(8,128)(2,1)}, bf16[768,576]{1,0:T(8,128)(2,1)S(1)}, u32[]{:S(2)}) copy-start(bf16[768,576]{1,0:T(8,128)(2,1)S(1)} %all_gather.31) | copy-start | bytes 2654212
  160.9 6.5 copy-start.5
  209.6 41.3 %all-to-all-start = ((bf16[4,768,192]{1,2,0:T(8,128)(2,1)}), bf16[4,768,192]{1,2,0:T(8,128)(2,1)S(1)}, u32[]{:S(2)}, u32[]{:S(2)}) async-start(bf16[4,768,192]{1,2,0:T(8,128)(2,1)} %copy.101), calls=%async_computation | async-start | bytes 2359296 | tf_op jit(solution)/shard_map/all_to_all | solution.py:441
  214.5 3.3 copy-start.24
  214.5 3.3 copy-start.25
  312.4 6.9 copy-start.9
  315.0 31.2 %all-to-all-start.1 = ((bf16[4,768,192]{1,2,0:T(8,128)(2,1)}), bf16[4,768,192]{1,2,0:T(8,128)(2,1)}, u32[]{:S(2)}, u32[]{:S(2)}) async-start(bf16[4,768,192]{1,2,0:T(8,128)(2,1)} %copy.104), calls=%async_computation.1 | async-start | bytes 2359296 | tf_op jit(solution)/shard_map/all_to_all | solution.py:451
  319.2 199.3 %reduce-scatter.9.cloned.1.call-start = ((), (), s32[]{:S(2)}) async-start(), calls=%async_computation.10 | async-start | bytes 1622016 | tf_op jit(solution)/shard_map/reduce_scatter | solution.py:458
  326.4 226.5 %all-reduce.6.cloned.1.call-start = ((), (), s32[]{:S(2)}) async-start(), calls=%async_computation.12 | async-start | bytes 344064
  368.9 43.2 %copy-start.12 = (bf16[768,576]{0,1:T(8,128)(2,1)S(1)}, bf16[768,576]{0,1:T(8,128)(2,1)}, u32[]{:S(2)}) copy-start(bf16[768,576]{0,1:T(8,128)(2,1)} %copy.111) | copy-start | bytes 2654212
  412.1 6.7 copy-start.2
  420.4 174.0 %reduce-scatter.7.cloned.1.call-start = ((), (), s32[]{:S(2)}) async-start(), calls=%async_computation.9 | async-start | bytes 1105920 | tf_op jit(solution)/shard_map/reduce_scatter | solution.py:484
  422.1 259.7 %reduce-scatter.5.cloned.1.call-start = ((), (), s32[]{:S(2)}) async-start(), calls=%async_computation.8 | async-start | bytes 5898240 | tf_op jit(solution)/shard_map/reduce_scatter | solution.py:477
  446.3 378.2 %reduce-scatter.11.cloned.1.call-start = ((), (), s32[]{:S(2)}) async-start(), calls=%async_computation.11 | async-start | bytes 9732096 | tf_op jit(solution)/shard_map/reduce_scatter | solution.py:457
  517.4 164.4 %copy-start.4 = (f32[768,768]{1,0:T(8,128)S(1)}, f32[768,768]{1,0:T(8,128)}, u32[]{:S(2)}) copy-start(f32[768,768]{1,0:T(8,128)} %copy-done.3) | copy-start | bytes 7077892
  685.0 143.6 %copy-start.1 = (bf16[192,192]{1,0:T(8,128)(2,1)S(1)}, bf16[192,192]{1,0:T(8,128)(2,1)}, u32[]{:S(2)}) copy-start(bf16[192,192]{1,0:T(8,128)(2,1)} %param.18) | copy-start | bytes 221188
  (13 other events, 23.2 us)
Sparse Core Ops, SparseCore 0:
  12.9 92.0 all-gather.6
  108.4 86.1 all-gather.8
  326.5 97.5 reduce-scatter.8
  430.1 122.7 all-reduce.5
  556.5 37.7 reduce-scatter.6
  596.5 85.2 reduce-scatter.4
  687.7 136.6 reduce-scatter.10
